TPU v7x, 128 devices: a whole 4x4x4 slice. The times are simulated.
128 devices in a mesh: rows: 4 (over y_hi, core), cols: 4 (over z), heads: 8 (over x, y_lo).
Axes of the slice: x: 4, y: 4 (y_hi: 2, y_lo: 2; y = y_hi * 2 + y_lo), z: 4, core: 2. Of those that a mesh axis runs over, the one named last changes fastest.
Arguments:
- tokens: bfloat16 [16384, 1024], P(('rows', 'cols'), 'heads'), may hold values from -8 to 8
- ln_gain: float32 [1024], replicated, may hold values from 0.1 to 1.9
- w_qkv: bfloat16 [3, 1024, 1024], P(None, None, 'heads'), may hold values from -1 to 1
- w_out: bfloat16 [1024, 1024], P('heads'), may hold values from -0.1875 to 0.1875
- out_bias: float32 [1024], P('heads'), may hold values from -3 to 3
Outputs:
- mixed: bfloat16 [16384, 1024], P(('rows', 'cols'), 'heads')
All inputs are finite; a program needn't handle non-finite values.
Results may differ from a plain program's by a relative error of at most 0.0095.
Values may be sent and summed in bfloat16 or wider, within the bound.
No kernel may reach another device: no remote copies, remote signals or barrier semaphores. Data moves between devices by JAX's collectives and lax.ppermute only.
A program may use at most 64 MiB of HBM per device.

v0:
```python
import functools

import jax
import jax.numpy as jnp
from jax import lax
from jax.experimental import pallas as pl
from jax.experimental.pallas import tpu as pltpu
from jax.sharding import PartitionSpec as P


D = 1024
HD = 64
LOG2E = 1.4426950408889634
QSCALE = LOG2E / HD**0.5
CAP = 2.0**60
AXES = ("rows", "cols", "heads")
bf16 = jnp.bfloat16
f32 = jnp.float32


def perm(move):
    pairs = []
    for i in range(128):
        here = dict(x=(i % 8) // 2, yl=i % 2, z=(i // 8) % 4, yh=i // 64, c=(i // 32) % 2)
        to = {**here, **move(here)}
        pairs.append((i, ((to["yh"] * 2 + to["c"]) * 4 + to["z"]) * 8 + to["x"] * 2 + to["yl"]))
    return pairs


Z_UP = perm(lambda d: dict(z=(d["z"] + 1) % 4))
Z_DOWN = perm(lambda d: dict(z=(d["z"] - 1) % 4))
Z_BY_CORE = perm(lambda d: dict(z=(d["z"] + 1 - 2 * d["c"]) % 4))
Z_FAR = perm(lambda d: dict(z=(d["z"] + 2) % 4))
YH_SWAP = perm(lambda d: dict(yh=1 - d["yh"]))
YL_SWAP = perm(lambda d: dict(yl=1 - d["yl"]))
CORE_SWAP = perm(lambda d: dict(c=1 - d["c"]))
X_UP = perm(lambda d: dict(x=(d["x"] + 1) % 4))
X_DOWN = perm(lambda d: dict(x=(d["x"] - 1) % 4))
X_FAR = perm(lambda d: dict(x=(d["x"] + 2) % 4))


def send(x, pairs):
    return lax.ppermute(x, AXES, pairs)


def vmem():
    return pl.BlockSpec(memory_space=pltpu.VMEM)


def hbm():
    return pl.BlockSpec(memory_space=pltpu.HBM)


def smem():
    return pl.BlockSpec(memory_space=pltpu.SMEM)


def project_kernel(ids_ref, *refs):
    x_refs = refs[:7]
    halves = refs[7:9]
    gain_ref, w_ref, kv_ref, q_ref, out_ref, qout_ref, n_even, n_odd = refs[9:]
    tok = x_refs[0].shape[0]
    step = 128
    half = tok // 2
    par = ids_ref[8]
    lane = lax.broadcasted_iota(jnp.int32, (step, 128), 1)
    low = lane < HD

    def norm(t, n_ref):
        for part in range(2):
            for r in range(0, step, 32):
                rows = slice(part * half + t * step + r, part * half + t * step + r + 32)
                parts = [x_ref[rows, :].astype(f32) for x_ref in x_refs]
                parts.append(halves[part][t * step + r : t * step + r + 32, :].astype(f32))
                total = parts[0]
                for p in parts[1:]:
                    total = total + p
                mean = jnp.sum(total, axis=1, keepdims=True) * (1.0 / D)
                cs = [p - mean for p in parts]
                sq = cs[0] * cs[0]
                for c in cs[1:]:
                    sq = sq + c * c
                var = jnp.sum(sq, axis=1, keepdims=True) * (1.0 / D)
                inv = lax.rsqrt(var + 1e-06)
                for h in range(8):
                    to = slice(part * step + r, part * step + r + 32)
                    n_ref[ids_ref[h], to] = (cs[h] * inv * gain_ref[ids_ref[h]]).astype(bf16)

    def one(t, n_ref):
        normed = jnp.concatenate([n_ref[h] for h in range(8)], axis=1)
        qk = jnp.dot(normed, jnp.concatenate([w_ref[0], w_ref[1]], axis=1), preferred_element_type=f32)
        v = jnp.dot(normed, w_ref[2], preferred_element_type=f32)
        k0, k1 = qk[:step, 128:], qk[step:, 128:]
        first = jnp.where(low, k0, pltpu.roll(k1, HD, 1))
        second = jnp.where(low, pltpu.roll(k0, HD, 1), k1)
        rows = slice(t * step, (t + 1) * step)
        kv_ref[rows, :] = jnp.where(par > 0, second, first).astype(bf16)
        out_ref[rows, :] = jnp.where(par > 0, first, second).astype(bf16)
        for part in range(2):
            own = slice(part * step, (part + 1) * step)
            block = (part * (half // step) + t) * HD
            vt = v[own].T
            vkeep = jnp.where(par > 0, vt[HD:], vt[:HD])
            vgive = jnp.where(par > 0, vt[:HD], vt[HD:])
            to = slice(half + block, half + block + HD)
            kv_ref[to, :] = vkeep.astype(bf16)
            out_ref[to, :] = vgive.astype(bf16)
            qt = (qk[own, :128] * QSCALE).T
            qkeep = jnp.where(par > 0, qt[HD:], qt[:HD])
            qgive = jnp.where(par > 0, qt[:HD], qt[HD:])
            q_ref[block : block + HD, :] = qkeep.astype(bf16)
            qout_ref[block : block + HD, :] = qgive.astype(bf16)

    bufs = (n_even, n_odd)
    trips = half // step
    norm(0, bufs[0])
    for t in range(trips):
        if t + 1 < trips:
            norm(t + 1, bufs[(t + 1) % 2])
        one(t, bufs[t % 2])


def stage_kernel(*refs):
    sems = refs[-1]
    count = len(refs) // 2
    copies = [pltpu.make_async_copy(refs[n], refs[count + n], sems.at[n]) for n in range(count)]
    for c in copies:
        c.start()
    for c in copies:
        c.wait()


def stage(*arrays):
    arrays = [pltpu.with_memory_space_constraint(a, pltpu.HBM) for a in arrays]
    return pl.pallas_call(
        stage_kernel,
        out_shape=[jax.ShapeDtypeStruct(a.shape, a.dtype) for a in arrays],
        in_specs=[hbm() for a in arrays],
        out_specs=[vmem() for a in arrays],
        scratch_shapes=[pltpu.SemaphoreType.DMA((len(arrays),))],
        compiler_params=pltpu.CompilerParams(vmem_limit_bytes=2 << 20),
        name="stage",
    )(*arrays)


def project(ids, blocks, gain, w):
    tok = blocks[0].shape[0]
    return pl.pallas_call(
        project_kernel,
        out_shape=(
            jax.ShapeDtypeStruct((tok, 128), bf16),
            jax.ShapeDtypeStruct((tok // 2, 128), bf16),
            jax.ShapeDtypeStruct((tok, 128), bf16),
            jax.ShapeDtypeStruct((tok // 2, 128), bf16),
        ),
        in_specs=[smem()] + [vmem()] * 11,
        out_specs=(vmem(), vmem(), vmem(), vmem()),
        scratch_shapes=[
            pltpu.VMEM((8, 256, 128), bf16),
            pltpu.VMEM((8, 256, 128), bf16),
        ],
        compiler_params=pltpu.CompilerParams(vmem_limit_bytes=12 << 20),
        name="project",
    )(ids, *blocks, gain, w)


def attend_kernel(*refs, npieces, windows, offset, first, outs, bq, unroll, ahead):
    pieces = refs[:npieces]
    qs = refs[npieces : npieces + len(windows)]
    rest = list(refs[npieces + len(windows) :])
    if not first:
        acc_in, m_in = rest[:2]
        rest = rest[2:]
    out_refs = rest[:outs]
    rest = rest[outs:]
    acc_ref, m_ref, q2, s = rest
    tiles = [(p, r) for p in pieces for r in range(0, p.shape[0], 1024)]
    nkb = len(tiles)
    nqb = q2.shape[0]
    per = bq // 128
    zero = jnp.zeros((HD, bq), bf16)
    jb = 0
    for q, (start, count) in zip(qs, windows):
        for j in range(count // HD // per):
            blocks = [q[start + (j * per + b) * HD : start + (j * per + b + 1) * HD, :] for b in range(per)]
            block = jnp.concatenate(blocks, axis=1)
            q2[jb, 0, 0:HD] = block
            q2[jb, 0, HD:] = zero
            q2[jb, 1, 0:HD] = zero
            q2[jb, 1, HD:] = block
            jb += 1

    if first:
        for j in range(nqb):
            top = jnp.dot(tiles[0][0][0:128], q2[j, 0], preferred_element_type=f32)
            m_ref[j] = jnp.max(top, axis=0, keepdims=True)
    else:
        for j in range(nqb):
            m_ref[j] = m_in[offset + j]

    def reset(j, _):
        acc_ref[j] = jnp.zeros(acc_ref.shape[1:], f32) if first else acc_in[offset + j]
        return 0

    lax.fori_loop(0, nqb, reset, 0)

    blocks = unroll // nkb
    units = [(d, i, c, g) for d in range(blocks) for i in range(nkb) for c in range(4) for g in range(bq // 256)]

    def unit(j, i, c, g):
        piece, row = tiles[i]
        half, at = c // 2, row + (c % 2) * 256
        k = piece[at : at + 256, :]
        return jnp.dot(k, q2[j, half, :, g * 256 : (g + 1) * 256], preferred_element_type=f32)

    def values(i, c):
        piece, row = tiles[i]
        at = [row + 512 + (c * 2 + b) * HD for b in range(2)]
        return jnp.concatenate([piece[r : r + HD, :] for r in at], axis=1)

    def trip(h):
        base = h * blocks
        then = jnp.where(base + blocks < nqb, base + blocks, 0)
        todo = [s[n] for n in range(ahead)]
        order = [(base + d, i, c, g) for d, i, c, g in units[ahead:]]
        order += [(then + d, i, c, g) for d, i, c, g in units[:ahead]]
        state = {}
        for n, (d, i, c, g) in enumerate(units):
            made = unit(*order[n])
            if n < len(units) - ahead:
                todo.append(made)
            else:
                s[n - (len(units) - ahead)] = made
            at = slice(g * 256, (g + 1) * 256)
            if (d, g) not in state:
                state[d, g] = [acc_ref[base + d, :HD, at], acc_ref[base + d, HD:, at], m_ref[base + d, :, at]]
            acc, den, top = state[d, g]
            p = jnp.exp2(todo[n] - top)
            den = den + jnp.sum(p.reshape(32, 8, 256), axis=0)
            acc = acc + jnp.dot(values(i, c), p.astype(bf16), preferred_element_type=f32)
            state[d, g] = [acc, den, top]
            if i == nkb - 1 and c == 3:
                acc_ref[base + d, :HD, at] = acc
                acc_ref[base + d, HD:, at] = den

    def exact(j, _):
        top = jnp.full((1, bq), -jnp.inf, f32) if first else m_in[offset + j]
        for piece, row in tiles:
            for half in range(2):

                def widen(r, top, piece=piece, row=row, half=half):
                    k = piece[pl.ds(pl.multiple_of(row + r * 128, 128), 128), :]
                    part = jnp.dot(k, q2[j, half], preferred_element_type=f32)
                    return jnp.maximum(top, jnp.max(part, axis=0, keepdims=True))

                top = lax.fori_loop(0, 4, widen, top)
        if first:
            acc_ref[j] = jnp.zeros(acc_ref.shape[1:], f32)
        else:
            acc_ref[j] = acc_in[offset + j] * jnp.exp2(m_in[offset + j] - top)
        m_ref[j] = top
        return 0

    def sweep(turn):
        @pl.when(turn > 0)
        def _():
            lax.fori_loop(0, nqb, exact, 0)

        for n in range(ahead):
            s[n] = unit(*units[n])

        def some(h, _):
            trip(h)
            return 0

        lax.fori_loop(0, nqb // blocks, some, 0)
        den = acc_ref[:, HD:, :]
        fine = jnp.min(jnp.where(den < CAP, 1.0, 0.0)) > 0.5
        return jnp.where(jnp.logical_or(turn > 0, fine), 2, 1)

    lax.while_loop(lambda turn: turn < 2, sweep, 0)

    for n, out_ref in enumerate(out_refs):
        for j in range(nqb // outs):
            a = acc_ref[n * (nqb // outs) + j]
            o = (a[0:HD] * (1.0 / jnp.sum(a[HD:], axis=0, keepdims=True))).astype(bf16)
            for b in range(per):
                out_ref[(j * per + b) * HD : (j * per + b + 1) * HD, :] = o[:, b * 128 : (b + 1) * 128]


def attend(pieces, qs, state=None, offset=0, outs=0, bq=512, unroll=8, ahead=4):
    windows = tuple(w for q, w in qs)
    nkeys = sum(p.shape[0] for p in pieces)
    nqueries = sum(count for start, count in windows) * 2
    nqb = nqueries // bq
    acc_shape = (nqb, HD + 8, bq)
    m_shape = (nqb, 1, bq)
    scratch = [
        pltpu.VMEM((nqb, 2, 128, bq), bf16),
        pltpu.VMEM((max(ahead, 1), 256, 256), f32),
    ]
    if outs:
        out_shape = [jax.ShapeDtypeStruct((nqueries // 2 // outs, 128), bf16)] * outs
        out_specs = [vmem()] * outs
        scratch = [pltpu.VMEM(acc_shape, f32), pltpu.VMEM(m_shape, f32)] + scratch
    else:
        out_shape = (jax.ShapeDtypeStruct(acc_shape, f32), jax.ShapeDtypeStruct(m_shape, f32))
        out_specs = (vmem(), vmem())
    args = [*pieces, *(q for q, w in qs)] + ([] if state is None else list(state))
    flops = 4 * nkeys * nqueries * 128
    return pl.pallas_call(
        functools.partial(
            attend_kernel, npieces=len(pieces), windows=windows, offset=offset, first=state is None, outs=outs, bq=bq, unroll=unroll, ahead=ahead
        ),
        out_shape=out_shape,
        in_specs=[vmem()] * len(args),
        out_specs=out_specs,
        scratch_shapes=scratch,
        compiler_params=pltpu.CompilerParams(vmem_limit_bytes=16 << 20),
        cost_estimate=pl.CostEstimate(flops=flops, transcendentals=nkeys * nqueries, bytes_accessed=nkeys * 256),
    )(*args)


def columns_of(att_refs, t, swap):
    kept, back, peer_kept, peer_back = att_refs
    at = pl.ds(pl.multiple_of(t * HD, HD), HD)
    cols = []
    for mine, other in ((kept, back), (peer_kept, peer_back)):
        a, b = mine[at, :], other[at, :]
        cols += [jnp.where(swap, b, a), jnp.where(swap, a, b)]
    return jnp.concatenate(cols, axis=0).T


def weights_for(pos_ref, own_ref, peer_ref, w_ref, steps):
    for n, b in enumerate(steps):
        cols = pl.ds(pl.multiple_of((((pos_ref[0] + b) % 4) * 2 + pos_ref[1]) * 128, 128), 128)
        w_ref[0:128, n * 128 : (n + 1) * 128] = own_ref[:, cols]
        w_ref[128:256, n * 128 : (n + 1) * 128] = peer_ref[:, cols]


def far_kernel(pos_ref, *refs):
    att_refs, (own_ref, peer_ref, lo_ref, hi_ref, t_ref, w_ref) = refs[:4], refs[4:]
    weights_for(pos_ref, own_ref, peer_ref, w_ref, (2,))
    swap = pos_ref[2] > 0
    count = att_refs[0].shape[0] // HD
    for t in range(count):
        rows = columns_of(att_refs, t, swap)
        t_ref[t] = rows
        out = jnp.dot(rows, w_ref[...], preferred_element_type=f32).astype(bf16)
        half = (lo_ref, hi_ref)[t // (count // 2)]
        to = (t % (count // 2)) * 128
        half[to : to + 128, :] = out


def mix_far(pos, att, own, peer):
    tok = att[0].shape[0] * 2
    return pl.pallas_call(
        far_kernel,
        out_shape=[jax.ShapeDtypeStruct((tok // 2, 128), bf16)] * 2
        + [jax.ShapeDtypeStruct((tok // 128, 128, 256), bf16)],
        in_specs=[smem()] + [vmem()] * 6,
        out_specs=[vmem()] * 3,
        scratch_shapes=[pltpu.VMEM((256, 128), bf16)],
        compiler_params=pltpu.CompilerParams(vmem_limit_bytes=6 << 20),
        name="mix_far",
    )(pos, *att, own, peer)


def mix_kernel(pos_ref, rows_ref, own_ref, peer_ref, x_ref, bias_ref, base_ref, up_ref, down_ref, w_ref):
    weights_for(pos_ref, own_ref, peer_ref, w_ref, (0, 1, 3))

    def one(t, _):
        out = jnp.dot(rows_ref[t], w_ref[...], preferred_element_type=f32)
        to = pl.ds(pl.multiple_of(t * 128, 128), 128)
        base_ref[to, :] = out[:, :128] + x_ref[to, :].astype(f32) + bias_ref[...]
        up_ref[to, :] = out[:, 128:256].astype(bf16)
        down_ref[to, :] = out[:, 256:].astype(bf16)
        return 0

    lax.fori_loop(0, rows_ref.shape[0], one, 0, unroll=4)


def mix(pos, rows, own, peer, x, bias):
    return pl.pallas_call(
        mix_kernel,
        out_shape=[jax.ShapeDtypeStruct(x.shape, f32)] + [jax.ShapeDtypeStruct(x.shape, bf16)] * 2,
        in_specs=[smem()] + [vmem()] * 5,
        out_specs=[vmem()] * 3,
        scratch_shapes=[pltpu.VMEM((256, 384), bf16)],
        compiler_params=pltpu.CompilerParams(vmem_limit_bytes=6 << 20),
        name="mix",
    )(pos, rows, own, peer, x, bias)


def join_kernel(up_ref, down_ref, lo_ref, hi_ref, upo_ref, downo_ref):
    half = lo_ref.shape[0]
    upo_ref[:half] = (up_ref[:half].astype(f32) + lo_ref[...].astype(f32)).astype(bf16)
    upo_ref[half:] = up_ref[half:]
    downo_ref[:half] = down_ref[:half]
    downo_ref[half:] = (down_ref[half:].astype(f32) + hi_ref[...].astype(f32)).astype(bf16)


def join(up, down, lo, hi):
    return pl.pallas_call(
        join_kernel,
        out_shape=[jax.ShapeDtypeStruct(up.shape, bf16)] * 2,
        in_specs=[vmem()] * 4,
        out_specs=[vmem()] * 2,
        compiler_params=pltpu.CompilerParams(vmem_limit_bytes=6 << 20),
        name="join",
    )(up, down, lo, hi)


def per_device(tokens, ln_gain, w_qkv, w_out, out_bias):
    rows = lax.axis_index("rows")
    heads = lax.axis_index("heads")
    yh = rows // 2
    x = heads // 2
    yl = heads % 2
    tok = tokens.shape[0]

    by_y = send(tokens, YL_SWAP)
    by_up = send(tokens, X_UP)
    by_down = send(tokens, X_DOWN)
    y_up = send(by_up, YL_SWAP)
    y_down = send(by_down, YL_SWAP)
    y_far = send(by_y, X_FAR)
    far_lo = send(by_up[: tok // 2], X_UP)
    far_hi = send(by_down[tok // 2 :], X_DOWN)
    held, w_held, bias = stage(tokens, w_qkv, out_bias.reshape(1, 128))
    blocks = (held, by_up, by_down, by_y, y_up, y_down, y_far, far_lo, far_hi)
    xs = jnp.stack([x, (x + 3) % 4, (x + 1) % 4, (x + 2) % 4])
    ids = jnp.concatenate([xs[:3] * 2 + yl, xs * 2 + 1 - yl, xs[3:] * 2 + yl, yh.reshape(1)]).astype(jnp.int32)

    kv, q, give, give_q = project(ids, blocks, ln_gain.reshape(8, 1, 128), w_held)
    kf = send(give, YH_SWAP)
    q_far = send(give_q, YH_SWAP)
    k_other = send(kv, CORE_SWAP)
    k_up = send(kv, Z_UP)
    k_down = send(kv, Z_DOWN)
    f_other = send(kf, CORE_SWAP)
    f_ring = send(jnp.concatenate([kf, f_other], axis=0), Z_BY_CORE)
    qs = ((q_far, (0, tok // 2)), (q, (0, tok // 2)))
    state = attend((kv, kf, k_other, f_other), qs)
    k_up, k_down, f_ring, w_send, state = lax.optimization_barrier((k_up, k_down, f_ring, w_out, state))
    far = jnp.concatenate([jnp.where(rows % 2 > 0, k_down, k_up), f_ring[:tok]], axis=0)
    far = send(far, Z_BY_CORE)
    ring = (k_up, k_down, f_ring)
    ring = ring + tuple(send(p, CORE_SWAP) for p in ring)
    w_peer = send(w_send, YL_SWAP)
    state_far = attend(ring, qs[:1], state)
    ends = (far, send(far, CORE_SWAP))
    (att_far,) = attend(ends, qs[:1], state_far, outs=1)
    back = send(att_far, YH_SWAP)
    q_own, att_far = lax.optimization_barrier((q, att_far))
    qs_own = ((q_own, (0, tok // 2)),)
    state_own = attend(ring, qs_own, state, offset=2)
    peer_back = send(back, YL_SWAP)
    (att,) = attend(ends, qs_own, state_own, outs=1)
    peer = send(att, YL_SWAP)
    pos = jnp.stack([x, yl, yh]).astype(jnp.int32)
    lo, hi, att_rows = mix_far(pos, (att, back, peer, peer_back), w_out, w_peer)
    lo = send(lo, X_UP)
    hi = send(hi, X_DOWN)
    base, up, down = mix(pos, att_rows, w_out, w_peer, tokens, bias)
    up, down = join(up, down, lo, hi)
    up = send(up, X_UP)
    down = send(down, X_DOWN)
    return (base + up.astype(f32) + down.astype(f32)).astype(bf16)


def solution(mesh):
    return jax.shard_map(
        per_device,
        mesh=mesh,
        in_specs=(
            P(("rows", "cols"), "heads"),
            P(),
            P(None, None, "heads"),
            P("heads", None),
            P("heads"),
        ),
        out_specs=P(("rows", "cols"), "heads"),
        check_vma=False,
    )
```

profile of v0, /device:TPU:0, one launch (start us, length us, event | category | flops | bytes accessed | tf_op | source)
XLA Modules:
  0.0 141.2 jit_solution(4966532272558309954)
XLA Ops:
  4.9 4.5 %collective-permute-done.refs_1_ = bf16[1024,128]{1,0:T(8,128)(2,1)S(1)} collective-permute-done((bf16[1024,128]{1,0:T(8,128)(2,1)}, bf16[1024,128]{1,0:T(8,128)(2,1)S(1)}, u32[]{:S(2)}, u32[]{:S(2)}) %collective-permute-start) | collective-permute-done | bytes 262176 | tf_op jit(solution)/shard_map/ppermute | solution.py:43
  11.4 2.5 %collective-permute-start.5 = (bf16[1024,128]{1,0:T(8,128)(2,1)S(1)}, bf16[1024,128]{1,0:T(8,128)(2,1)S(1)}, u32[]{:S(2)}, u32[]{:S(2)}) collective-permute-start(bf16[1024,128]{1,0:T(8,128)(2,1)S(1)} %collective-permute-done.2.refs_3_), channel_id=1, source_target_pairs={{0,4},{1,5},{2,6},{3,7},{4,0},{5,1},{6,2},{7,3},{8,12},{9,13},{10,... | collective-permute-start | bytes 786440 | tf_op jit(solution)/shard_map/ppermute | solution.py:43
  15.1 2.2 %collective-permute-start.7 = (bf16[512,128]{1,0:T(8,128)(2,1)S(1)}, bf16[512,128]{1,0:T(8,128)(2,1)S(1)}, u32[]{:S(2)}, u32[]{:S(2)}) collective-permute-start(bf16[512,128]{1,0:T(8,128)(2,1)S(1)} %slice.15), channel_id=1, source_target_pairs={{0,6},{1,7},{2,0},{3,1},{4,2},{5,3},{6,4},{7,5},{8,14},{9,15},{10,... | collective-permute-start | bytes 393224 | tf_op jit(solution)/shard_map/ppermute | solution.py:43
  18.8 3.7 %collective-permute-done.6.refs_7_ = bf16[512,128]{1,0:T(8,128)(2,1)S(1)} collective-permute-done((bf16[512,128]{1,0:T(8,128)(2,1)S(1)}, bf16[512,128]{1,0:T(8,128)(2,1)S(1)}, u32[]{:S(2)}, u32[]{:S(2)}) %collective-permute-start.6) | collective-permute-done | bytes 131104 | tf_op jit(solution)/shard_map/ppermute | solution.py:43
  22.5 3.1 %project.1 = (bf16[1024,128]{1,0:T(8,128)(2,1)S(1)}, bf16[512,128]{1,0:T(8,128)(2,1)S(1)}, bf16[1024,128]{1,0:T(8,128)(2,1)S(1)}, bf16[512,128]{1,0:T(8,128)(2,1)S(1)}) custom-call(s32[9]{0:T(128)S(1)} %pad_add_fusion.1.ids_ref, bf16[1024,128]{1,0:T(8,128)(2,1)S(1)} %get-tuple-element.33.refs_0_, bf16[1024,128]{1,0:T(8,128)(2,1)S(1)} %collective-permute-done.refs_1_, ...), custom_call_target="tpu_custom_call" | custom-call | tf_op jit(solution)/shard_map/project/pallas_call | solution.py:148
  25.6 3.4 %collective-permute-start.10 = (bf16[1024,128]{1,0:T(8,128)(2,1)S(1)}, bf16[1024,128]{1,0:T(8,128)(2,1)S(1)}, u32[]{:S(2)}, u32[]{:S(2)}) collective-permute-start(bf16[1024,128]{1,0:T(8,128)(2,1)S(1)} %get-tuple-element.36), channel_id=1, source_target_pairs={{0,64},{1,65},{2,66},{3,67},{4,68},{5,69},{6,70},{7,71},{8,72},{9,... | collective-permute-start | bytes 786440 | tf_op jit(solution)/shard_map/ppermute | solution.py:43
  28.9 5.9 %collective-permute-done.10.refs_1_ = bf16[1024,128]{1,0:T(8,128)(2,1)S(1)} collective-permute-done((bf16[1024,128]{1,0:T(8,128)(2,1)S(1)}, bf16[1024,128]{1,0:T(8,128)(2,1)S(1)}, u32[]{:S(2)}, u32[]{:S(2)}) %collective-permute-start.10) | collective-permute-done | bytes 262176 | tf_op jit(solution)/shard_map/ppermute | solution.py:43
  35.4 3.2 %collective-permute-start.14 = (bf16[512,128]{1,0:T(8,128)(2,1)S(1)}, bf16[512,128]{1,0:T(8,128)(2,1)S(1)}, u32[]{:S(2)}, u32[]{:S(2)}) collective-permute-start(bf16[512,128]{1,0:T(8,128)(2,1)S(1)} %get-tuple-element.37), channel_id=1, source_target_pairs={{0,64},{1,65},{2,66},{3,67},{4,68},{5,69},{6,70},{7,71},{8,72},{9,... | collective-permute-start | bytes 393224 | tf_op jit(solution)/shard_map/ppermute | solution.py:43
  38.6 2.0 %collective-permute-start.12 = (bf16[2048,128]{1,0:T(8,128)(2,1)S(1)}, bf16[2048,128]{1,0:T(8,128)(2,1)S(1)}, u32[]{:S(2)}, u32[]{:S(2)}) collective-permute-start(bf16[2048,128]{1,0:T(8,128)(2,1)S(1)} %pad_maximum_fusion), channel_id=1, source_target_pairs={{0,8},{1,9},{2,10},{3,11},{4,12},{5,13},{6,14},{7,15},{8,16},{9,17... | collective-permute-start | bytes 1572872 | tf_op jit(solution)/shard_map/ppermute | solution.py:43
  40.6 1.9 %collective-permute-start.8 = (bf16[1024,128]{1,0:T(8,128)(2,1)S(1)}, bf16[1024,128]{1,0:T(8,128)(2,1)S(1)}, u32[]{:S(2)}, u32[]{:S(2)}) collective-permute-start(bf16[1024,128]{1,0:T(8,128)(2,1)S(1)} %get-tuple-element.35.refs_0_), channel_id=1, source_target_pairs={{0,8},{1,9},{2,10},{3,11},{4,12},{5,13},{6,14},{7,15},{8,16},{9,17... | collective-permute-start | bytes 786440 | tf_op jit(solution)/shard_map/ppermute | solution.py:43
  43.9 36.3 %shard_map.55 = (f32[4,72,512]{2,1,0:T(8,128)S(1)}, f32[4,1,512]{2,1,0:T(1,128)S(1)}) custom-call(bf16[1024,128]{1,0:T(8,128)(2,1)S(1)} %get-tuple-element.35.refs_0_, bf16[1024,128]{1,0:T(8,128)(2,1)S(1)} %collective-permute-done.10.refs_1_, bf16[1024,128]{1,0:T(8,128)(2,1)S(1)} %collective-permute-done.13.refs_2_, ...), custom_call_target="tpu_custom_call" | custom-call | flops 4294967296 | bytes 1048576 | tf_op jit(solution)/shard_map/pallas_call | solution.py:311
  82.4 8.6 %collective-permute-done.15.refs_0_ = bf16[2048,128]{1,0:T(8,128)(2,1)S(1)} collective-permute-done((bf16[2048,128]{1,0:T(8,128)(2,1)S(1)}, bf16[2048,128]{1,0:T(8,128)(2,1)S(1)}, u32[]{:S(2)}, u32[]{:S(2)}) %collective-permute-start.15) | collective-permute-done | bytes 524320 | tf_op jit(solution)/shard_map/ppermute | solution.py:43
  91.9 6.3 %shard_map.56 = (f32[2,72,512]{2,1,0:T(8,128)S(1)}, f32[2,1,512]{2,1,0:T(1,128)S(1)}) custom-call(bf16[1024,128]{1,0:T(8,128)(2,1)S(1)} %collective-permute-done.8.refs_0_, bf16[1024,128]{1,0:T(8,128)(2,1)S(1)} %collective-permute-done.9.refs_1_, bf16[2048,128]{1,0:T(8,128)(2,1)S(1)} %collective-permute-done.12.refs_2_, ...), custom_call_target="tpu_custom_call" | custom-call | flops 4294967296 | bytes 2097152 | tf_op jit(solution)/shard_map/pallas_call | solution.py:311
  98.2 3.2 %shard_map.57 = bf16[512,128]{1,0:T(8,128)(2,1)S(1)} custom-call(bf16[2048,128]{1,0:T(8,128)(2,1)S(1)} %collective-permute-done.15.refs_0_, bf16[2048,128]{1,0:T(8,128)(2,1)S(1)} %collective-permute-done.16.refs_1_, bf16[512,128]{1,0:T(8,128)(2,1)S(1)} %collective-permute-done.14.refs_4_.refs_6_.refs_2_, f32[2,72,512]{2,1,0:T(8,128)S(1)} %get-tuple-element.46.refs_3_, ...), custom_call_target="tpu_custom_call" | custom-call | flops 2147483648 | bytes 1048576 | tf_op jit(solution)/shard_map/pallas_call | solution.py:311
  101.4 3.2 %collective-permute-start.20 = (bf16[512,128]{1,0:T(8,128)(2,1)S(1)}, bf16[512,128]{1,0:T(8,128)(2,1)S(1)}, u32[]{:S(2)}, u32[]{:S(2)}) collective-permute-start(bf16[512,128]{1,0:T(8,128)(2,1)S(1)} %shard_map.57), channel_id=1, source_target_pairs={{0,64},{1,65},{2,66},{3,67},{4,68},{5,69},{6,70},{7,71},{8,72},{9,... | collective-permute-start | bytes 393224 | tf_op jit(solution)/shard_map/ppermute | solution.py:43
  104.5 6.3 %shard_map.58 = (f32[2,72,512]{2,1,0:T(8,128)S(1)}, f32[2,1,512]{2,1,0:T(1,128)S(1)}) custom-call(bf16[1024,128]{1,0:T(8,128)(2,1)S(1)} %collective-permute-done.8.refs_0_, bf16[1024,128]{1,0:T(8,128)(2,1)S(1)} %collective-permute-done.9.refs_1_, bf16[2048,128]{1,0:T(8,128)(2,1)S(1)} %collective-permute-done.12.refs_2_, ...), custom_call_target="tpu_custom_call" | custom-call | flops 4294967296 | bytes 2097152 | tf_op jit(solution)/shard_map/pallas_call | solution.py:311
  110.8 3.2 %shard_map.59.refs_0_ = bf16[512,128]{1,0:T(8,128)(2,1)S(1)} custom-call(bf16[2048,128]{1,0:T(8,128)(2,1)S(1)} %collective-permute-done.15.refs_0_, bf16[2048,128]{1,0:T(8,128)(2,1)S(1)} %collective-permute-done.16.refs_1_, bf16[512,128]{1,0:T(8,128)(2,1)S(1)} %get-tuple-element.48.refs_5_.refs_6_.refs_2_, f32[2,72,512]{2,1,0:T(8,128)S(1)} %get-tuple-element.49.refs_3_, ...), custom_call_target="tpu_custom_call" | custom-call | flops 2147483648 | bytes 1048576 | tf_op jit(solution)/shard_map/pallas_call | solution.py:311
  114.1 2.0 %collective-permute-start.22 = (bf16[512,128]{1,0:T(8,128)(2,1)S(1)}, bf16[512,128]{1,0:T(8,128)(2,1)S(1)}, u32[]{:S(2)}, u32[]{:S(2)}) collective-permute-start(bf16[512,128]{1,0:T(8,128)(2,1)S(1)} %collective-permute-done.20.refs_1_), channel_id=1, source_target_pairs={{0,1},{1,0},{2,3},{3,2},{4,5},{5,4},{6,7},{7,6},{8,9},{9,8},{10,11... | collective-permute-start | bytes 393224 | tf_op jit(solution)/shard_map/ppermute | solution.py:43
  116.2 4.3 %collective-permute-done.21.refs_2_ = bf16[512,128]{1,0:T(8,128)(2,1)S(1)} collective-permute-done((bf16[512,128]{1,0:T(8,128)(2,1)S(1)}, bf16[512,128]{1,0:T(8,128)(2,1)S(1)}, u32[]{:S(2)}, u32[]{:S(2)}) %collective-permute-start.21) | collective-permute-done | bytes 131104 | tf_op jit(solution)/shard_map/ppermute | solution.py:43
  120.5 1.8 %collective-permute-done.22.refs_3_ = bf16[512,128]{1,0:T(8,128)(2,1)S(1)} collective-permute-done((bf16[512,128]{1,0:T(8,128)(2,1)S(1)}, bf16[512,128]{1,0:T(8,128)(2,1)S(1)}, u32[]{:S(2)}, u32[]{:S(2)}) %collective-permute-start.22) | collective-permute-done | bytes 131104 | tf_op jit(solution)/shard_map/ppermute | solution.py:43
  123.3 3.1 %collective-permute-start.25 = (bf16[512,128]{1,0:T(8,128)(2,1)S(1)}, bf16[512,128]{1,0:T(8,128)(2,1)S(1)}, u32[]{:S(2)}, u32[]{:S(2)}) collective-permute-start(bf16[512,128]{1,0:T(8,128)(2,1)S(1)} %get-tuple-element.58), channel_id=1, source_target_pairs={{0,6},{1,7},{2,0},{3,1},{4,2},{5,3},{6,4},{7,5},{8,14},{9,15},{10,... | collective-permute-start | bytes 393224 | tf_op jit(solution)/shard_map/ppermute | solution.py:43
  129.5 3.3 %collective-permute-start.27 = (bf16[1024,128]{1,0:T(8,128)(2,1)S(1)}, bf16[1024,128]{1,0:T(8,128)(2,1)S(1)}, u32[]{:S(2)}, u32[]{:S(2)}) collective-permute-start(bf16[1024,128]{1,0:T(8,128)(2,1)S(1)} %get-tuple-element.60), channel_id=1, source_target_pairs={{0,6},{1,7},{2,0},{3,1},{4,2},{5,3},{6,4},{7,5},{8,14},{9,15},{10,... | collective-permute-start | bytes 786440 | tf_op jit(solution)/shard_map/ppermute | solution.py:43
  132.8 3.9 %collective-permute-done.27 = bf16[1024,128]{1,0:T(8,128)(2,1)S(1)} collective-permute-done((bf16[1024,128]{1,0:T(8,128)(2,1)S(1)}, bf16[1024,128]{1,0:T(8,128)(2,1)S(1)}, u32[]{:S(2)}, u32[]{:S(2)}) %collective-permute-start.27) | collective-permute-done | bytes 262176 | tf_op jit(solution)/shard_map/ppermute | solution.py:43
  136.7 3.7 %collective-permute-done.26 = bf16[1024,128]{1,0:T(8,128)(2,1)S(1)} collective-permute-done((bf16[1024,128]{1,0:T(8,128)(2,1)S(1)}, bf16[1024,128]{1,0:T(8,128)(2,1)S(1)}, u32[]{:S(2)}, u32[]{:S(2)}) %collective-permute-start.26) | collective-permute-done | bytes 262176 | tf_op jit(solution)/shard_map/ppermute | solution.py:43
  (59 shorter events, 19.7 us)
Async XLA Ops:
  0.0 9.4 %collective-permute-start = (bf16[1024,128]{1,0:T(8,128)(2,1)}, bf16[1024,128]{1,0:T(8,128)(2,1)S(1)}, u32[]{:S(2)}, u32[]{:S(2)}) collective-permute-start(bf16[1024,128]{1,0:T(8,128)(2,1)} %x_ref.1), channel_id=1, source_target_pairs={{0,2},{1,3},{2,4},{3,5},{4,6},{5,7},{6,0},{7,1},{8,10},{9,11},{10,... | collective-permute-start | bytes 786440 | tf_op jit(solution)/shard_map/ppermute | solution.py:43
  1.6 9.6 %collective-permute-start.1 = (bf16[1024,128]{1,0:T(8,128)(2,1)}, bf16[1024,128]{1,0:T(8,128)(2,1)S(1)}, u32[]{:S(2)}, u32[]{:S(2)}) collective-permute-start(bf16[1024,128]{1,0:T(8,128)(2,1)} %x_ref.1), channel_id=1, source_target_pairs={{0,6},{1,7},{2,0},{3,1},{4,2},{5,3},{6,4},{7,5},{8,14},{9,15},{10,... | collective-permute-start | bytes 786440 | tf_op jit(solution)/shard_map/ppermute | solution.py:43
  3.2 8.2 %collective-permute-start.2 = (bf16[1024,128]{1,0:T(8,128)(2,1)}, bf16[1024,128]{1,0:T(8,128)(2,1)S(1)}, u32[]{:S(2)}, u32[]{:S(2)}) collective-permute-start(bf16[1024,128]{1,0:T(8,128)(2,1)} %x_ref.1), channel_id=1, source_target_pairs={{0,1},{1,0},{2,3},{3,2},{4,5},{5,4},{6,7},{7,6},{8,9},{9,8},{10,11... | collective-permute-start | bytes 786440 | tf_op jit(solution)/shard_map/ppermute | solution.py:43
  9.4 13.1 %collective-permute-start.3 = (bf16[1024,128]{1,0:T(8,128)(2,1)S(1)}, bf16[1024,128]{1,0:T(8,128)(2,1)S(1)}, u32[]{:S(2)}, u32[]{:S(2)}) collective-permute-start(bf16[1024,128]{1,0:T(8,128)(2,1)S(1)} %collective-permute-done.refs_1_), channel_id=1, source_target_pairs={{0,1},{1,0},{2,3},{3,2},{4,5},{5,4},{6,7},{7,6},{8,9},{9,8},{10,11... | collective-permute-start | bytes 786440 | tf_op jit(solution)/shard_map/ppermute | solution.py:43
  11.2 11.3 %collective-permute-start.4 = (bf16[1024,128]{1,0:T(8,128)(2,1)S(1)}, bf16[1024,128]{1,0:T(8,128)(2,1)S(1)}, u32[]{:S(2)}, u32[]{:S(2)}) collective-permute-start(bf16[1024,128]{1,0:T(8,128)(2,1)S(1)} %collective-permute-done.1.refs_2_), channel_id=1, source_target_pairs={{0,1},{1,0},{2,3},{3,2},{4,5},{5,4},{6,7},{7,6},{8,9},{9,8},{10,11... | collective-permute-start | bytes 786440 | tf_op jit(solution)/shard_map/ppermute | solution.py:43
  11.4 11.1 %collective-permute-start.5 = (bf16[1024,128]{1,0:T(8,128)(2,1)S(1)}, bf16[1024,128]{1,0:T(8,128)(2,1)S(1)}, u32[]{:S(2)}, u32[]{:S(2)}) collective-permute-start(bf16[1024,128]{1,0:T(8,128)(2,1)S(1)} %collective-permute-done.2.refs_3_), channel_id=1, source_target_pairs={{0,4},{1,5},{2,6},{3,7},{4,0},{5,1},{6,2},{7,3},{8,12},{9,13},{10,... | collective-permute-start | bytes 786440 | tf_op jit(solution)/shard_map/ppermute | solution.py:43
  14.0 8.5 %collective-permute-start.6 = (bf16[512,128]{1,0:T(8,128)(2,1)S(1)}, bf16[512,128]{1,0:T(8,128)(2,1)S(1)}, u32[]{:S(2)}, u32[]{:S(2)}) collective-permute-start(bf16[512,128]{1,0:T(8,128)(2,1)S(1)} %slice.14), channel_id=1, source_target_pairs={{0,2},{1,3},{2,4},{3,5},{4,6},{5,7},{6,0},{7,1},{8,10},{9,11},{10,... | collective-permute-start | bytes 393224 | tf_op jit(solution)/shard_map/ppermute | solution.py:43
  15.1 7.3 %collective-permute-start.7 = (bf16[512,128]{1,0:T(8,128)(2,1)S(1)}, bf16[512,128]{1,0:T(8,128)(2,1)S(1)}, u32[]{:S(2)}, u32[]{:S(2)}) collective-permute-start(bf16[512,128]{1,0:T(8,128)(2,1)S(1)} %slice.15), channel_id=1, source_target_pairs={{0,6},{1,7},{2,0},{3,1},{4,2},{5,3},{6,4},{7,5},{8,14},{9,15},{10,... | collective-permute-start | bytes 393224 | tf_op jit(solution)/shard_map/ppermute | solution.py:43
  25.6 9.3 %collective-permute-start.10 = (bf16[1024,128]{1,0:T(8,128)(2,1)S(1)}, bf16[1024,128]{1,0:T(8,128)(2,1)S(1)}, u32[]{:S(2)}, u32[]{:S(2)}) collective-permute-start(bf16[1024,128]{1,0:T(8,128)(2,1)S(1)} %get-tuple-element.36), channel_id=1, source_target_pairs={{0,64},{1,65},{2,66},{3,67},{4,68},{5,69},{6,70},{7,71},{8,72},{9,... | collective-permute-start | bytes 786440 | tf_op jit(solution)/shard_map/ppermute | solution.py:43
  34.8 9.0 %collective-permute-start.13 = (bf16[1024,128]{1,0:T(8,128)(2,1)S(1)}, bf16[1024,128]{1,0:T(8,128)(2,1)S(1)}, u32[]{:S(2)}, u32[]{:S(2)}) collective-permute-start(bf16[1024,128]{1,0:T(8,128)(2,1)S(1)} %get-tuple-element.35.refs_0_), channel_id=1, source_target_pairs={{0,32},{1,33},{2,34},{3,35},{4,36},{5,37},{6,38},{7,39},{8,40},{9,... | collective-permute-start | bytes 786440 | tf_op jit(solution)/shard_map/ppermute | solution.py:43
  35.4 8.5 %collective-permute-start.14 = (bf16[512,128]{1,0:T(8,128)(2,1)S(1)}, bf16[512,128]{1,0:T(8,128)(2,1)S(1)}, u32[]{:S(2)}, u32[]{:S(2)}) collective-permute-start(bf16[512,128]{1,0:T(8,128)(2,1)S(1)} %get-tuple-element.37), channel_id=1, source_target_pairs={{0,64},{1,65},{2,66},{3,67},{4,68},{5,69},{6,70},{7,71},{8,72},{9,... | collective-permute-start | bytes 393224 | tf_op jit(solution)/shard_map/ppermute | solution.py:43
  38.6 41.5 %collective-permute-start.12 = (bf16[2048,128]{1,0:T(8,128)(2,1)S(1)}, bf16[2048,128]{1,0:T(8,128)(2,1)S(1)}, u32[]{:S(2)}, u32[]{:S(2)}) collective-permute-start(bf16[2048,128]{1,0:T(8,128)(2,1)S(1)} %pad_maximum_fusion), channel_id=1, source_target_pairs={{0,8},{1,9},{2,10},{3,11},{4,12},{5,13},{6,14},{7,15},{8,16},{9,17... | collective-permute-start | bytes 1572872 | tf_op jit(solution)/shard_map/ppermute | solution.py:43
  40.6 39.5 %collective-permute-start.8 = (bf16[1024,128]{1,0:T(8,128)(2,1)S(1)}, bf16[1024,128]{1,0:T(8,128)(2,1)S(1)}, u32[]{:S(2)}, u32[]{:S(2)}) collective-permute-start(bf16[1024,128]{1,0:T(8,128)(2,1)S(1)} %get-tuple-element.35.refs_0_), channel_id=1, source_target_pairs={{0,8},{1,9},{2,10},{3,11},{4,12},{5,13},{6,14},{7,15},{8,16},{9,17... | collective-permute-start | bytes 786440 | tf_op jit(solution)/shard_map/ppermute | solution.py:43
  42.5 37.6 %collective-permute-start.9 = (bf16[1024,128]{1,0:T(8,128)(2,1)S(1)}, bf16[1024,128]{1,0:T(8,128)(2,1)S(1)}, u32[]{:S(2)}, u32[]{:S(2)}) collective-permute-start(bf16[1024,128]{1,0:T(8,128)(2,1)S(1)} %get-tuple-element.35.refs_0_), channel_id=1, source_target_pairs={{0,24},{1,25},{2,26},{3,27},{4,28},{5,29},{6,30},{7,31},{8,0},{9,1... | collective-permute-start | bytes 786440 | tf_op jit(solution)/shard_map/ppermute | solution.py:43
  80.3 10.6 %collective-permute-start.15 = (bf16[2048,128]{1,0:T(8,128)(2,1)S(1)}, bf16[2048,128]{1,0:T(8,128)(2,1)S(1)}, u32[]{:S(2)}, u32[]{:S(2)}) collective-permute-start(bf16[2048,128]{1,0:T(8,128)(2,1)S(1)} %pad_maximum_fusion.1), channel_id=1, source_target_pairs={{0,8},{1,9},{2,10},{3,11},{4,12},{5,13},{6,14},{7,15},{8,16},{9,17... | collective-permute-start | bytes 1572872 | tf_op jit(solution)/shard_map/ppermute | solution.py:43
  81.3 10.6 %collective-permute-start.19 = (bf16[2048,128]{1,0:T(8,128)(2,1)S(1)}, bf16[2048,128]{1,0:T(8,128)(2,1)S(1)}, u32[]{:S(2)}, u32[]{:S(2)}) collective-permute-start(bf16[2048,128]{1,0:T(8,128)(2,1)S(1)} %collective-permute-done.12.refs_2_), channel_id=1, source_target_pairs={{0,32},{1,33},{2,34},{3,35},{4,36},{5,37},{6,38},{7,39},{8,40},{9,... | collective-permute-start | bytes 1572872 | tf_op jit(solution)/shard_map/ppermute | solution.py:43
  81.9 10.0 %collective-permute-start.17 = (bf16[1024,128]{1,0:T(8,128)(2,1)S(1)}, bf16[1024,128]{1,0:T(8,128)(2,1)S(1)}, u32[]{:S(2)}, u32[]{:S(2)}) collective-permute-start(bf16[1024,128]{1,0:T(8,128)(2,1)S(1)} %collective-permute-done.8.refs_0_), channel_id=1, source_target_pairs={{0,32},{1,33},{2,34},{3,35},{4,36},{5,37},{6,38},{7,39},{8,40},{9,... | collective-permute-start | bytes 786440 | tf_op jit(solution)/shard_map/ppermute | solution.py:43
  81.9 10.0 %collective-permute-start.18 = (bf16[1024,128]{1,0:T(8,128)(2,1)S(1)}, bf16[1024,128]{1,0:T(8,128)(2,1)S(1)}, u32[]{:S(2)}, u32[]{:S(2)}) collective-permute-start(bf16[1024,128]{1,0:T(8,128)(2,1)S(1)} %collective-permute-done.9.refs_1_), channel_id=1, source_target_pairs={{0,32},{1,33},{2,34},{3,35},{4,36},{5,37},{6,38},{7,39},{8,40},{9,... | collective-permute-start | bytes 786440 | tf_op jit(solution)/shard_map/ppermute | solution.py:43
  91.0 7.2 %collective-permute-start.16 = (bf16[2048,128]{1,0:T(8,128)(2,1)S(1)}, bf16[2048,128]{1,0:T(8,128)(2,1)S(1)}, u32[]{:S(2)}, u32[]{:S(2)}) collective-permute-start(bf16[2048,128]{1,0:T(8,128)(2,1)S(1)} %collective-permute-done.15.refs_0_), channel_id=1, source_target_pairs={{0,32},{1,33},{2,34},{3,35},{4,36},{5,37},{6,38},{7,39},{8,40},{9,... | collective-permute-start | bytes 1572872 | tf_op jit(solution)/shard_map/ppermute | solution.py:43
  91.0 25.2 %collective-permute-start.23 = (bf16[128,1024]{1,0:T(8,128)(2,1)S(1)}, bf16[128,1024]{1,0:T(8,128)(2,1)S(1)}, u32[]{:S(2)}, u32[]{:S(2)}) collective-permute-start(bf16[128,1024]{1,0:T(8,128)(2,1)S(1)} %copy-done.1), channel_id=1, source_target_pairs={{0,1},{1,0},{2,3},{3,2},{4,5},{5,4},{6,7},{7,6},{8,9},{9,8},{10,11... | collective-permute-start | bytes 786440 | tf_op jit(solution)/shard_map/ppermute | solution.py:43
  101.4 12.8 %collective-permute-start.20 = (bf16[512,128]{1,0:T(8,128)(2,1)S(1)}, bf16[512,128]{1,0:T(8,128)(2,1)S(1)}, u32[]{:S(2)}, u32[]{:S(2)}) collective-permute-start(bf16[512,128]{1,0:T(8,128)(2,1)S(1)} %shard_map.57), channel_id=1, source_target_pairs={{0,64},{1,65},{2,66},{3,67},{4,68},{5,69},{6,70},{7,71},{8,72},{9,... | collective-permute-start | bytes 393224 | tf_op jit(solution)/shard_map/ppermute | solution.py:43
  114.1 8.1 %collective-permute-start.22 = (bf16[512,128]{1,0:T(8,128)(2,1)S(1)}, bf16[512,128]{1,0:T(8,128)(2,1)S(1)}, u32[]{:S(2)}, u32[]{:S(2)}) collective-permute-start(bf16[512,128]{1,0:T(8,128)(2,1)S(1)} %collective-permute-done.20.refs_1_), channel_id=1, source_target_pairs={{0,1},{1,0},{2,3},{3,2},{4,5},{5,4},{6,7},{7,6},{8,9},{9,8},{10,11... | collective-permute-start | bytes 393224 | tf_op jit(solution)/shard_map/ppermute | solution.py:43
  129.5 7.2 %collective-permute-start.27 = (bf16[1024,128]{1,0:T(8,128)(2,1)S(1)}, bf16[1024,128]{1,0:T(8,128)(2,1)S(1)}, u32[]{:S(2)}, u32[]{:S(2)}) collective-permute-start(bf16[1024,128]{1,0:T(8,128)(2,1)S(1)} %get-tuple-element.60), channel_id=1, source_target_pairs={{0,6},{1,7},{2,0},{3,1},{4,2},{5,3},{6,4},{7,5},{8,14},{9,15},{10,... | collective-permute-start | bytes 786440 | tf_op jit(solution)/shard_map/ppermute | solution.py:43
  132.8 7.6 %collective-permute-start.26 = (bf16[1024,128]{1,0:T(8,128)(2,1)S(1)}, bf16[1024,128]{1,0:T(8,128)(2,1)S(1)}, u32[]{:S(2)}, u32[]{:S(2)}) collective-permute-start(bf16[1024,128]{1,0:T(8,128)(2,1)S(1)} %get-tuple-element.59), channel_id=1, source_target_pairs={{0,2},{1,3},{2,4},{3,5},{4,6},{5,7},{6,0},{7,1},{8,10},{9,11},{10,... | collective-permute-start | bytes 786440 | tf_op jit(solution)/shard_map/ppermute | solution.py:43
  (7 other events, 47.3 us)
where the time goes:
time: 141 us
  Pallas kernels  61.6 us (44%)
  starting transfers between devices  40 us (28%)
  waiting for transfers between devices  38.1 us (27%)
    pallas_call x5, Pallas kernels, attend(): pl.pallas_call(functools.partial(attend_kernel, npieces=len(pieces), wind...  55.2 us
    ppermute x28, starting transfers between devices, send(): return lax.ppermute(x, AXES, pairs)  40 us
    ppermute x28, waiting for transfers between devices, send(): return lax.ppermute(x, AXES, pairs)  38.1 us
    pallas_call x1, Pallas kernels, project(): pl.pallas_call(project_kernel, out_shape=(jax.ShapeDtypeStruct((tok, 128)...  3.05 us
  transfers between devices with their start and end apart: 28, of which 9 were waited for; matrix products, arithmetic and copies ran while one was open for 0% of the time, Pallas kernels for 41%

commit v1 on v0

--- a/solution.py
+++ b/solution.py
@@ -439,13 +439,14 @@
     k_up = send(kv, Z_UP)
     k_down = send(kv, Z_DOWN)
     f_other = send(kf, CORE_SWAP)
-    f_ring = send(jnp.concatenate([kf, f_other], axis=0), Z_BY_CORE)
+    f_up = send(kf, Z_UP)
+    f_down = send(kf, Z_DOWN)
     qs = ((q_far, (0, tok // 2)), (q, (0, tok // 2)))
     state = attend((kv, kf, k_other, f_other), qs)
-    k_up, k_down, f_ring, w_send, state = lax.optimization_barrier((k_up, k_down, f_ring, w_out, state))
-    far = jnp.concatenate([jnp.where(rows % 2 > 0, k_down, k_up), f_ring[:tok]], axis=0)
-    far = send(far, Z_BY_CORE)
-    ring = (k_up, k_down, f_ring)
+    k_up, k_down, f_up, f_down, w_send, state = lax.optimization_barrier((k_up, k_down, f_up, f_down, w_out, state))
+    chosen = jnp.where(rows % 2 > 0, jnp.stack([k_down, f_down]), jnp.stack([k_up, f_up]))
+    far = send(chosen.reshape(2 * tok, 128), Z_BY_CORE)
+    ring = (k_up, k_down, f_up, f_down)
     ring = ring + tuple(send(p, CORE_SWAP) for p in ring)
     w_peer = send(w_send, YL_SWAP)
     state_far = attend(ring, qs[:1], state)

time: 141 us -> 144 us (1.021)
  starting transfers between devices: 40 us -> 42.9 us
    ppermute x28 -> x30, starting transfers between devices: 40 us -> 42.9 us  [send(): return lax.ppermute(x, AXES, pairs)]
    ppermute x28 -> x30, waiting for transfers between devices: 38.1 us -> 38.3 us  [send(): return lax.ppermute(x, AXES, pairs)]
  transfers between devices with their start and end apart: 28 -> 30, of which waited for: 9 -> 10; matrix products, arithmetic and copies ran while one was open for 0% -> 0% of each run, Pallas kernels for 41% -> 40%
where the time goes in v1:
time: 144 us
  Pallas kernels  61.7 us (43%)
  starting transfers between devices  42.9 us (30%)
  waiting for transfers between devices  38.3 us (27%)
    pallas_call x5, Pallas kernels, attend(): pl.pallas_call(functools.partial(attend_kernel, npieces=len(pieces), wind...  55.2 us
    ppermute x30, starting transfers between devices, send(): return lax.ppermute(x, AXES, pairs)  42.9 us
    ppermute x30, waiting for transfers between devices, send(): return lax.ppermute(x, AXES, pairs)  38.3 us
    pallas_call x1, Pallas kernels, project(): pl.pallas_call(project_kernel, out_shape=(jax.ShapeDtypeStruct((tok, 128)...  3.05 us
  transfers between devices with their start and end apart: 30, of which 10 were waited for; matrix products, arithmetic and copies ran while one was open for 0% of the time, Pallas kernels for 40%

profile of v1, /device:TPU:0, one launch (start us, length us, event | category | flops | bytes accessed | tf_op | source)
XLA Modules:
  0.0 144.3 jit_solution(12216176891012463979)
XLA Ops:
  4.9 4.5 %collective-permute-done.refs_1_ = bf16[1024,128]{1,0:T(8,128)(2,1)S(1)} collective-permute-done((bf16[1024,128]{1,0:T(8,128)(2,1)}, bf16[1024,128]{1,0:T(8,128)(2,1)S(1)}, u32[]{:S(2)}, u32[]{:S(2)}) %collective-permute-start) | collective-permute-done | bytes 262176 | tf_op jit(solution)/shard_map/ppermute | solution.py:43
  11.4 2.5 %collective-permute-start.5 = (bf16[1024,128]{1,0:T(8,128)(2,1)S(1)}, bf16[1024,128]{1,0:T(8,128)(2,1)S(1)}, u32[]{:S(2)}, u32[]{:S(2)}) collective-permute-start(bf16[1024,128]{1,0:T(8,128)(2,1)S(1)} %collective-permute-done.2.refs_3_), channel_id=1, source_target_pairs={{0,4},{1,5},{2,6},{3,7},{4,0},{5,1},{6,2},{7,3},{8,12},{9,13},{10,... | collective-permute-start | bytes 786440 | tf_op jit(solution)/shard_map/ppermute | solution.py:43
  15.1 2.2 %collective-permute-start.7 = (bf16[512,128]{1,0:T(8,128)(2,1)S(1)}, bf16[512,128]{1,0:T(8,128)(2,1)S(1)}, u32[]{:S(2)}, u32[]{:S(2)}) collective-permute-start(bf16[512,128]{1,0:T(8,128)(2,1)S(1)} %slice.11), channel_id=1, source_target_pairs={{0,6},{1,7},{2,0},{3,1},{4,2},{5,3},{6,4},{7,5},{8,14},{9,15},{10,... | collective-permute-start | bytes 393224 | tf_op jit(solution)/shard_map/ppermute | solution.py:43
  18.8 3.7 %collective-permute-done.6.refs_7_ = bf16[512,128]{1,0:T(8,128)(2,1)S(1)} collective-permute-done((bf16[512,128]{1,0:T(8,128)(2,1)S(1)}, bf16[512,128]{1,0:T(8,128)(2,1)S(1)}, u32[]{:S(2)}, u32[]{:S(2)}) %collective-permute-start.6) | collective-permute-done | bytes 131104 | tf_op jit(solution)/shard_map/ppermute | solution.py:43
  22.5 3.1 %project.1 = (bf16[1024,128]{1,0:T(8,128)(2,1)S(1)}, bf16[512,128]{1,0:T(8,128)(2,1)S(1)}, bf16[1024,128]{1,0:T(8,128)(2,1)S(1)}, bf16[512,128]{1,0:T(8,128)(2,1)S(1)}) custom-call(s32[9]{0:T(128)S(1)} %pad_add_fusion.1.ids_ref, bf16[1024,128]{1,0:T(8,128)(2,1)S(1)} %get-tuple-element.34.refs_0_, bf16[1024,128]{1,0:T(8,128)(2,1)S(1)} %collective-permute-done.refs_1_, ...), custom_call_target="tpu_custom_call" | custom-call | tf_op jit(solution)/shard_map/project/pallas_call | solution.py:148
  25.6 3.4 %collective-permute-start.10 = (bf16[1024,128]{1,0:T(8,128)(2,1)S(1)}, bf16[1024,128]{1,0:T(8,128)(2,1)S(1)}, u32[]{:S(2)}, u32[]{:S(2)}) collective-permute-start(bf16[1024,128]{1,0:T(8,128)(2,1)S(1)} %get-tuple-element.37), channel_id=1, source_target_pairs={{0,64},{1,65},{2,66},{3,67},{4,68},{5,69},{6,70},{7,71},{8,72},{9,... | collective-permute-start | bytes 786440 | tf_op jit(solution)/shard_map/ppermute | solution.py:43
  28.9 5.9 %collective-permute-done.10.refs_1_ = bf16[1024,128]{1,0:T(8,128)(2,1)S(1)} collective-permute-done((bf16[1024,128]{1,0:T(8,128)(2,1)S(1)}, bf16[1024,128]{1,0:T(8,128)(2,1)S(1)}, u32[]{:S(2)}, u32[]{:S(2)}) %collective-permute-start.10) | collective-permute-done | bytes 262176 | tf_op jit(solution)/shard_map/ppermute | solution.py:43
  34.8 3.2 %collective-permute-start.15 = (bf16[512,128]{1,0:T(8,128)(2,1)S(1)}, bf16[512,128]{1,0:T(8,128)(2,1)S(1)}, u32[]{:S(2)}, u32[]{:S(2)}) collective-permute-start(bf16[512,128]{1,0:T(8,128)(2,1)S(1)} %get-tuple-element.38), channel_id=1, source_target_pairs={{0,64},{1,65},{2,66},{3,67},{4,68},{5,69},{6,70},{7,71},{8,72},{9,... | collective-permute-start | bytes 393224 | tf_op jit(solution)/shard_map/ppermute | solution.py:43
  40.0 2.1 %collective-permute-start.9 = (bf16[1024,128]{1,0:T(8,128)(2,1)S(1)}, bf16[1024,128]{1,0:T(8,128)(2,1)S(1)}, u32[]{:S(2)}, u32[]{:S(2)}) collective-permute-start(bf16[1024,128]{1,0:T(8,128)(2,1)S(1)} %get-tuple-element.36.refs_0_), channel_id=1, source_target_pairs={{0,24},{1,25},{2,26},{3,27},{4,28},{5,29},{6,30},{7,31},{8,0},{9,1... | collective-permute-start | bytes 786440 | tf_op jit(solution)/shard_map/ppermute | solution.py:43
  44.2 2.1 %collective-permute-start.12 = (bf16[1024,128]{1,0:T(8,128)(2,1)S(1)}, bf16[1024,128]{1,0:T(8,128)(2,1)S(1)}, u32[]{:S(2)}, u32[]{:S(2)}) collective-permute-start(bf16[1024,128]{1,0:T(8,128)(2,1)S(1)} %collective-permute-done.10.refs_1_), channel_id=1, source_target_pairs={{0,24},{1,25},{2,26},{3,27},{4,28},{5,29},{6,30},{7,31},{8,0},{9,1... | collective-permute-start | bytes 786440 | tf_op jit(solution)/shard_map/ppermute | solution.py:43
  46.3 36.3 %shard_map.55 = (f32[4,72,512]{2,1,0:T(8,128)S(1)}, f32[4,1,512]{2,1,0:T(1,128)S(1)}) custom-call(bf16[1024,128]{1,0:T(8,128)(2,1)S(1)} %get-tuple-element.36.refs_0_, bf16[1024,128]{1,0:T(8,128)(2,1)S(1)} %collective-permute-done.10.refs_1_, bf16[1024,128]{1,0:T(8,128)(2,1)S(1)} %collective-permute-done.13.refs_2_, ...), custom_call_target="tpu_custom_call" | custom-call | flops 4294967296 | bytes 1048576 | tf_op jit(solution)/shard_map/pallas_call | solution.py:311
  84.2 9.0 %collective-permute-done.16.refs_0_ = bf16[2048,128]{1,0:T(8,128)(2,1)S(1)} collective-permute-done((bf16[2048,128]{1,0:T(8,128)(2,1)S(1)}, bf16[2048,128]{1,0:T(8,128)(2,1)S(1)}, u32[]{:S(2)}, u32[]{:S(2)}) %collective-permute-start.16) | collective-permute-done | bytes 524320 | tf_op jit(solution)/shard_map/ppermute | solution.py:43
  93.2 2.0 %collective-permute-start.25 = (bf16[128,1024]{1,0:T(8,128)(2,1)S(1)}, bf16[128,1024]{1,0:T(8,128)(2,1)S(1)}, u32[]{:S(2)}, u32[]{:S(2)}) collective-permute-start(bf16[128,1024]{1,0:T(8,128)(2,1)S(1)} %copy-done.1), channel_id=1, source_target_pairs={{0,1},{1,0},{2,3},{3,2},{4,5},{5,4},{6,7},{7,6},{8,9},{9,8},{10,11... | collective-permute-start | bytes 786440 | tf_op jit(solution)/shard_map/ppermute | solution.py:43
  95.2 6.3 %shard_map.56 = (f32[2,72,512]{2,1,0:T(8,128)S(1)}, f32[2,1,512]{2,1,0:T(1,128)S(1)}) custom-call(bf16[1024,128]{1,0:T(8,128)(2,1)S(1)} %collective-permute-done.8.refs_0_, bf16[1024,128]{1,0:T(8,128)(2,1)S(1)} %collective-permute-done.9.refs_1_, bf16[1024,128]{1,0:T(8,128)(2,1)S(1)} %collective-permute-done.11.refs_2_, ...), custom_call_target="tpu_custom_call" | custom-call | flops 4294967296 | bytes 2097152 | tf_op jit(solution)/shard_map/pallas_call | solution.py:311
  101.6 3.2 %shard_map.57 = bf16[512,128]{1,0:T(8,128)(2,1)S(1)} custom-call(bf16[2048,128]{1,0:T(8,128)(2,1)S(1)} %collective-permute-done.16.refs_0_, bf16[2048,128]{1,0:T(8,128)(2,1)S(1)} %collective-permute-done.17.refs_1_, bf16[512,128]{1,0:T(8,128)(2,1)S(1)} %collective-permute-done.15.refs_4_.refs_8_.refs_2_, f32[2,72,512]{2,1,0:T(8,128)S(1)} %get-tuple-element.48.refs_3_, ...), custom_call_target="tpu_custom_call" | custom-call | flops 2147483648 | bytes 1048576 | tf_op jit(solution)/shard_map/pallas_call | solution.py:311
  104.7 3.2 %collective-permute-start.22 = (bf16[512,128]{1,0:T(8,128)(2,1)S(1)}, bf16[512,128]{1,0:T(8,128)(2,1)S(1)}, u32[]{:S(2)}, u32[]{:S(2)}) collective-permute-start(bf16[512,128]{1,0:T(8,128)(2,1)S(1)} %shard_map.57), channel_id=1, source_target_pairs={{0,64},{1,65},{2,66},{3,67},{4,68},{5,69},{6,70},{7,71},{8,72},{9,... | collective-permute-start | bytes 393224 | tf_op jit(solution)/shard_map/ppermute | solution.py:43
  108.0 6.3 %shard_map.58 = (f32[2,72,512]{2,1,0:T(8,128)S(1)}, f32[2,1,512]{2,1,0:T(1,128)S(1)}) custom-call(bf16[1024,128]{1,0:T(8,128)(2,1)S(1)} %collective-permute-done.8.refs_0_, bf16[1024,128]{1,0:T(8,128)(2,1)S(1)} %collective-permute-done.9.refs_1_, bf16[1024,128]{1,0:T(8,128)(2,1)S(1)} %collective-permute-done.11.refs_2_, ...), custom_call_target="tpu_custom_call" | custom-call | flops 4294967296 | bytes 2097152 | tf_op jit(solution)/shard_map/pallas_call | solution.py:311
  114.3 3.2 %shard_map.59.refs_0_ = bf16[512,128]{1,0:T(8,128)(2,1)S(1)} custom-call(bf16[2048,128]{1,0:T(8,128)(2,1)S(1)} %collective-permute-done.16.refs_0_, bf16[2048,128]{1,0:T(8,128)(2,1)S(1)} %collective-permute-done.17.refs_1_, bf16[512,128]{1,0:T(8,128)(2,1)S(1)} %get-tuple-element.50.refs_5_.refs_8_.refs_2_, f32[2,72,512]{2,1,0:T(8,128)S(1)} %get-tuple-element.51.refs_3_, ...), custom_call_target="tpu_custom_call" | custom-call | flops 2147483648 | bytes 1048576 | tf_op jit(solution)/shard_map/pallas_call | solution.py:311
  117.6 2.0 %collective-permute-start.24 = (bf16[512,128]{1,0:T(8,128)(2,1)S(1)}, bf16[512,128]{1,0:T(8,128)(2,1)S(1)}, u32[]{:S(2)}, u32[]{:S(2)}) collective-permute-start(bf16[512,128]{1,0:T(8,128)(2,1)S(1)} %collective-permute-done.22.refs_1_), channel_id=1, source_target_pairs={{0,1},{1,0},{2,3},{3,2},{4,5},{5,4},{6,7},{7,6},{8,9},{9,8},{10,11... | collective-permute-start | bytes 393224 | tf_op jit(solution)/shard_map/ppermute | solution.py:43
  119.7 4.3 %collective-permute-done.23.refs_2_ = bf16[512,128]{1,0:T(8,128)(2,1)S(1)} collective-permute-done((bf16[512,128]{1,0:T(8,128)(2,1)S(1)}, bf16[512,128]{1,0:T(8,128)(2,1)S(1)}, u32[]{:S(2)}, u32[]{:S(2)}) %collective-permute-start.23) | collective-permute-done | bytes 131104 | tf_op jit(solution)/shard_map/ppermute | solution.py:43
  126.5 3.1 %collective-permute-start.27 = (bf16[512,128]{1,0:T(8,128)(2,1)S(1)}, bf16[512,128]{1,0:T(8,128)(2,1)S(1)}, u32[]{:S(2)}, u32[]{:S(2)}) collective-permute-start(bf16[512,128]{1,0:T(8,128)(2,1)S(1)} %get-tuple-element.60), channel_id=1, source_target_pairs={{0,6},{1,7},{2,0},{3,1},{4,2},{5,3},{6,4},{7,5},{8,14},{9,15},{10,... | collective-permute-start | bytes 393224 | tf_op jit(solution)/shard_map/ppermute | solution.py:43
  132.7 3.3 %collective-permute-start.29 = (bf16[1024,128]{1,0:T(8,128)(2,1)S(1)}, bf16[1024,128]{1,0:T(8,128)(2,1)S(1)}, u32[]{:S(2)}, u32[]{:S(2)}) collective-permute-start(bf16[1024,128]{1,0:T(8,128)(2,1)S(1)} %get-tuple-element.62), channel_id=1, source_target_pairs={{0,6},{1,7},{2,0},{3,1},{4,2},{5,3},{6,4},{7,5},{8,14},{9,15},{10,... | collective-permute-start | bytes 786440 | tf_op jit(solution)/shard_map/ppermute | solution.py:43
  136.0 3.9 %collective-permute-done.29 = bf16[1024,128]{1,0:T(8,128)(2,1)S(1)} collective-permute-done((bf16[1024,128]{1,0:T(8,128)(2,1)S(1)}, bf16[1024,128]{1,0:T(8,128)(2,1)S(1)}, u32[]{:S(2)}, u32[]{:S(2)}) %collective-permute-start.29) | collective-permute-done | bytes 262176 | tf_op jit(solution)/shard_map/ppermute | solution.py:43
  139.8 3.7 %collective-permute-done.28 = bf16[1024,128]{1,0:T(8,128)(2,1)S(1)} collective-permute-done((bf16[1024,128]{1,0:T(8,128)(2,1)S(1)}, bf16[1024,128]{1,0:T(8,128)(2,1)S(1)}, u32[]{:S(2)}, u32[]{:S(2)}) %collective-permute-start.28) | collective-permute-done | bytes 262176 | tf_op jit(solution)/shard_map/ppermute | solution.py:43
  (60 shorter events, 21.8 us)
Async XLA Ops:
  0.0 9.4 %collective-permute-start = (bf16[1024,128]{1,0:T(8,128)(2,1)}, bf16[1024,128]{1,0:T(8,128)(2,1)S(1)}, u32[]{:S(2)}, u32[]{:S(2)}) collective-permute-start(bf16[1024,128]{1,0:T(8,128)(2,1)} %x_ref.1), channel_id=1, source_target_pairs={{0,2},{1,3},{2,4},{3,5},{4,6},{5,7},{6,0},{7,1},{8,10},{9,11},{10,... | collective-permute-start | bytes 786440 | tf_op jit(solution)/shard_map/ppermute | solution.py:43
  1.6 9.6 %collective-permute-start.1 = (bf16[1024,128]{1,0:T(8,128)(2,1)}, bf16[1024,128]{1,0:T(8,128)(2,1)S(1)}, u32[]{:S(2)}, u32[]{:S(2)}) collective-permute-start(bf16[1024,128]{1,0:T(8,128)(2,1)} %x_ref.1), channel_id=1, source_target_pairs={{0,6},{1,7},{2,0},{3,1},{4,2},{5,3},{6,4},{7,5},{8,14},{9,15},{10,... | collective-permute-start | bytes 786440 | tf_op jit(solution)/shard_map/ppermute | solution.py:43
  3.2 8.2 %collective-permute-start.2 = (bf16[1024,128]{1,0:T(8,128)(2,1)}, bf16[1024,128]{1,0:T(8,128)(2,1)S(1)}, u32[]{:S(2)}, u32[]{:S(2)}) collective-permute-start(bf16[1024,128]{1,0:T(8,128)(2,1)} %x_ref.1), channel_id=1, source_target_pairs={{0,1},{1,0},{2,3},{3,2},{4,5},{5,4},{6,7},{7,6},{8,9},{9,8},{10,11... | collective-permute-start | bytes 786440 | tf_op jit(solution)/shard_map/ppermute | solution.py:43
  9.4 13.1 %collective-permute-start.3 = (bf16[1024,128]{1,0:T(8,128)(2,1)S(1)}, bf16[1024,128]{1,0:T(8,128)(2,1)S(1)}, u32[]{:S(2)}, u32[]{:S(2)}) collective-permute-start(bf16[1024,128]{1,0:T(8,128)(2,1)S(1)} %collective-permute-done.refs_1_), channel_id=1, source_target_pairs={{0,1},{1,0},{2,3},{3,2},{4,5},{5,4},{6,7},{7,6},{8,9},{9,8},{10,11... | collective-permute-start | bytes 786440 | tf_op jit(solution)/shard_map/ppermute | solution.py:43
  11.2 11.3 %collective-permute-start.4 = (bf16[1024,128]{1,0:T(8,128)(2,1)S(1)}, bf16[1024,128]{1,0:T(8,128)(2,1)S(1)}, u32[]{:S(2)}, u32[]{:S(2)}) collective-permute-start(bf16[1024,128]{1,0:T(8,128)(2,1)S(1)} %collective-permute-done.1.refs_2_), channel_id=1, source_target_pairs={{0,1},{1,0},{2,3},{3,2},{4,5},{5,4},{6,7},{7,6},{8,9},{9,8},{10,11... | collective-permute-start | bytes 786440 | tf_op jit(solution)/shard_map/ppermute | solution.py:43
  11.4 11.1 %collective-permute-start.5 = (bf16[1024,128]{1,0:T(8,128)(2,1)S(1)}, bf16[1024,128]{1,0:T(8,128)(2,1)S(1)}, u32[]{:S(2)}, u32[]{:S(2)}) collective-permute-start(bf16[1024,128]{1,0:T(8,128)(2,1)S(1)} %collective-permute-done.2.refs_3_), channel_id=1, source_target_pairs={{0,4},{1,5},{2,6},{3,7},{4,0},{5,1},{6,2},{7,3},{8,12},{9,13},{10,... | collective-permute-start | bytes 786440 | tf_op jit(solution)/shard_map/ppermute | solution.py:43
  14.0 8.5 %collective-permute-start.6 = (bf16[512,128]{1,0:T(8,128)(2,1)S(1)}, bf16[512,128]{1,0:T(8,128)(2,1)S(1)}, u32[]{:S(2)}, u32[]{:S(2)}) collective-permute-start(bf16[512,128]{1,0:T(8,128)(2,1)S(1)} %slice.10), channel_id=1, source_target_pairs={{0,2},{1,3},{2,4},{3,5},{4,6},{5,7},{6,0},{7,1},{8,10},{9,11},{10,... | collective-permute-start | bytes 393224 | tf_op jit(solution)/shard_map/ppermute | solution.py:43
  25.6 9.3 %collective-permute-start.10 = (bf16[1024,128]{1,0:T(8,128)(2,1)S(1)}, bf16[1024,128]{1,0:T(8,128)(2,1)S(1)}, u32[]{:S(2)}, u32[]{:S(2)}) collective-permute-start(bf16[1024,128]{1,0:T(8,128)(2,1)S(1)} %get-tuple-element.37), channel_id=1, source_target_pairs={{0,64},{1,65},{2,66},{3,67},{4,68},{5,69},{6,70},{7,71},{8,72},{9,... | collective-permute-start | bytes 786440 | tf_op jit(solution)/shard_map/ppermute | solution.py:43
  28.9 15.3 %collective-permute-start.13 = (bf16[1024,128]{1,0:T(8,128)(2,1)S(1)}, bf16[1024,128]{1,0:T(8,128)(2,1)S(1)}, u32[]{:S(2)}, u32[]{:S(2)}) collective-permute-start(bf16[1024,128]{1,0:T(8,128)(2,1)S(1)} %get-tuple-element.36.refs_0_), channel_id=1, source_target_pairs={{0,32},{1,33},{2,34},{3,35},{4,36},{5,37},{6,38},{7,39},{8,40},{9,... | collective-permute-start | bytes 786440 | tf_op jit(solution)/shard_map/ppermute | solution.py:43
  34.8 11.5 %collective-permute-start.14 = (bf16[1024,128]{1,0:T(8,128)(2,1)S(1)}, bf16[1024,128]{1,0:T(8,128)(2,1)S(1)}, u32[]{:S(2)}, u32[]{:S(2)}) collective-permute-start(bf16[1024,128]{1,0:T(8,128)(2,1)S(1)} %collective-permute-done.10.refs_1_), channel_id=1, source_target_pairs={{0,32},{1,33},{2,34},{3,35},{4,36},{5,37},{6,38},{7,39},{8,40},{9,... | collective-permute-start | bytes 786440 | tf_op jit(solution)/shard_map/ppermute | solution.py:43
  38.1 44.5 %collective-permute-start.8 = (bf16[1024,128]{1,0:T(8,128)(2,1)S(1)}, bf16[1024,128]{1,0:T(8,128)(2,1)S(1)}, u32[]{:S(2)}, u32[]{:S(2)}) collective-permute-start(bf16[1024,128]{1,0:T(8,128)(2,1)S(1)} %get-tuple-element.36.refs_0_), channel_id=1, source_target_pairs={{0,8},{1,9},{2,10},{3,11},{4,12},{5,13},{6,14},{7,15},{8,16},{9,17... | collective-permute-start | bytes 786440 | tf_op jit(solution)/shard_map/ppermute | solution.py:43
  40.0 42.6 %collective-permute-start.9 = (bf16[1024,128]{1,0:T(8,128)(2,1)S(1)}, bf16[1024,128]{1,0:T(8,128)(2,1)S(1)}, u32[]{:S(2)}, u32[]{:S(2)}) collective-permute-start(bf16[1024,128]{1,0:T(8,128)(2,1)S(1)} %get-tuple-element.36.refs_0_), channel_id=1, source_target_pairs={{0,24},{1,25},{2,26},{3,27},{4,28},{5,29},{6,30},{7,31},{8,0},{9,1... | collective-permute-start | bytes 786440 | tf_op jit(solution)/shard_map/ppermute | solution.py:43
  42.3 40.3 %collective-permute-start.11 = (bf16[1024,128]{1,0:T(8,128)(2,1)S(1)}, bf16[1024,128]{1,0:T(8,128)(2,1)S(1)}, u32[]{:S(2)}, u32[]{:S(2)}) collective-permute-start(bf16[1024,128]{1,0:T(8,128)(2,1)S(1)} %collective-permute-done.10.refs_1_), channel_id=1, source_target_pairs={{0,8},{1,9},{2,10},{3,11},{4,12},{5,13},{6,14},{7,15},{8,16},{9,17... | collective-permute-start | bytes 786440 | tf_op jit(solution)/shard_map/ppermute | solution.py:43
  44.2 38.4 %collective-permute-start.12 = (bf16[1024,128]{1,0:T(8,128)(2,1)S(1)}, bf16[1024,128]{1,0:T(8,128)(2,1)S(1)}, u32[]{:S(2)}, u32[]{:S(2)}) collective-permute-start(bf16[1024,128]{1,0:T(8,128)(2,1)S(1)} %collective-permute-done.10.refs_1_), channel_id=1, source_target_pairs={{0,24},{1,25},{2,26},{3,27},{4,28},{5,29},{6,30},{7,31},{8,0},{9,1... | collective-permute-start | bytes 786440 | tf_op jit(solution)/shard_map/ppermute | solution.py:43
  82.7 10.5 %collective-permute-start.16 = (bf16[2048,128]{1,0:T(8,128)(2,1)S(1)}, bf16[2048,128]{1,0:T(8,128)(2,1)S(1)}, u32[]{:S(2)}, u32[]{:S(2)}) collective-permute-start(bf16[2048,128]{1,0:T(8,128)(2,1)S(1)} %bitcast.18), channel_id=1, source_target_pairs={{0,8},{1,9},{2,10},{3,11},{4,12},{5,13},{6,14},{7,15},{8,16},{9,17... | collective-permute-start | bytes 1572872 | tf_op jit(solution)/shard_map/ppermute | solution.py:43
  82.8 10.4 %collective-permute-start.18 = (bf16[1024,128]{1,0:T(8,128)(2,1)S(1)}, bf16[1024,128]{1,0:T(8,128)(2,1)S(1)}, u32[]{:S(2)}, u32[]{:S(2)}) collective-permute-start(bf16[1024,128]{1,0:T(8,128)(2,1)S(1)} %collective-permute-done.8.refs_0_), channel_id=1, source_target_pairs={{0,32},{1,33},{2,34},{3,35},{4,36},{5,37},{6,38},{7,39},{8,40},{9,... | collective-permute-start | bytes 786440 | tf_op jit(solution)/shard_map/ppermute | solution.py:43
  83.6 11.6 %collective-permute-start.19 = (bf16[1024,128]{1,0:T(8,128)(2,1)S(1)}, bf16[1024,128]{1,0:T(8,128)(2,1)S(1)}, u32[]{:S(2)}, u32[]{:S(2)}) collective-permute-start(bf16[1024,128]{1,0:T(8,128)(2,1)S(1)} %collective-permute-done.9.refs_1_), channel_id=1, source_target_pairs={{0,32},{1,33},{2,34},{3,35},{4,36},{5,37},{6,38},{7,39},{8,40},{9,... | collective-permute-start | bytes 786440 | tf_op jit(solution)/shard_map/ppermute | solution.py:43
  83.7 11.6 %collective-permute-start.20 = (bf16[1024,128]{1,0:T(8,128)(2,1)S(1)}, bf16[1024,128]{1,0:T(8,128)(2,1)S(1)}, u32[]{:S(2)}, u32[]{:S(2)}) collective-permute-start(bf16[1024,128]{1,0:T(8,128)(2,1)S(1)} %collective-permute-done.11.refs_2_), channel_id=1, source_target_pairs={{0,32},{1,33},{2,34},{3,35},{4,36},{5,37},{6,38},{7,39},{8,40},{9,... | collective-permute-start | bytes 786440 | tf_op jit(solution)/shard_map/ppermute | solution.py:43
  84.2 11.1 %collective-permute-start.21 = (bf16[1024,128]{1,0:T(8,128)(2,1)S(1)}, bf16[1024,128]{1,0:T(8,128)(2,1)S(1)}, u32[]{:S(2)}, u32[]{:S(2)}) collective-permute-start(bf16[1024,128]{1,0:T(8,128)(2,1)S(1)} %collective-permute-done.12.refs_3_), channel_id=1, source_target_pairs={{0,32},{1,33},{2,34},{3,35},{4,36},{5,37},{6,38},{7,39},{8,40},{9,... | collective-permute-start | bytes 786440 | tf_op jit(solution)/shard_map/ppermute | solution.py:43
  93.2 8.4 %collective-permute-start.17 = (bf16[2048,128]{1,0:T(8,128)(2,1)S(1)}, bf16[2048,128]{1,0:T(8,128)(2,1)S(1)}, u32[]{:S(2)}, u32[]{:S(2)}) collective-permute-start(bf16[2048,128]{1,0:T(8,128)(2,1)S(1)} %collective-permute-done.16.refs_0_), channel_id=1, source_target_pairs={{0,32},{1,33},{2,34},{3,35},{4,36},{5,37},{6,38},{7,39},{8,40},{9,... | collective-permute-start | bytes 1572872 | tf_op jit(solution)/shard_map/ppermute | solution.py:43
  93.2 26.5 %collective-permute-start.25 = (bf16[128,1024]{1,0:T(8,128)(2,1)S(1)}, bf16[128,1024]{1,0:T(8,128)(2,1)S(1)}, u32[]{:S(2)}, u32[]{:S(2)}) collective-permute-start(bf16[128,1024]{1,0:T(8,128)(2,1)S(1)} %copy-done.1), channel_id=1, source_target_pairs={{0,1},{1,0},{2,3},{3,2},{4,5},{5,4},{6,7},{7,6},{8,9},{9,8},{10,11... | collective-permute-start | bytes 786440 | tf_op jit(solution)/shard_map/ppermute | solution.py:43
  104.7 12.9 %collective-permute-start.22 = (bf16[512,128]{1,0:T(8,128)(2,1)S(1)}, bf16[512,128]{1,0:T(8,128)(2,1)S(1)}, u32[]{:S(2)}, u32[]{:S(2)}) collective-permute-start(bf16[512,128]{1,0:T(8,128)(2,1)S(1)} %shard_map.57), channel_id=1, source_target_pairs={{0,64},{1,65},{2,66},{3,67},{4,68},{5,69},{6,70},{7,71},{8,72},{9,... | collective-permute-start | bytes 393224 | tf_op jit(solution)/shard_map/ppermute | solution.py:43
  117.6 7.8 %collective-permute-start.24 = (bf16[512,128]{1,0:T(8,128)(2,1)S(1)}, bf16[512,128]{1,0:T(8,128)(2,1)S(1)}, u32[]{:S(2)}, u32[]{:S(2)}) collective-permute-start(bf16[512,128]{1,0:T(8,128)(2,1)S(1)} %collective-permute-done.22.refs_1_), channel_id=1, source_target_pairs={{0,1},{1,0},{2,3},{3,2},{4,5},{5,4},{6,7},{7,6},{8,9},{9,8},{10,11... | collective-permute-start | bytes 393224 | tf_op jit(solution)/shard_map/ppermute | solution.py:43
  136.0 7.6 %collective-permute-start.28 = (bf16[1024,128]{1,0:T(8,128)(2,1)S(1)}, bf16[1024,128]{1,0:T(8,128)(2,1)S(1)}, u32[]{:S(2)}, u32[]{:S(2)}) collective-permute-start(bf16[1024,128]{1,0:T(8,128)(2,1)S(1)} %get-tuple-element.61), channel_id=1, source_target_pairs={{0,2},{1,3},{2,4},{3,5},{4,6},{5,7},{6,0},{7,1},{8,10},{9,11},{10,... | collective-permute-start | bytes 786440 | tf_op jit(solution)/shard_map/ppermute | solution.py:43
  (9 other events, 65.0 us)
